TPU v7x, 32 devices: a whole 2x2x4 slice. The times are simulated.
32 devices in a mesh: frag: 2 (over x), grid: 16 (over z, y, core).
Axes of the slice: x: 2, y: 2, z: 4, core: 2. Of those that a mesh axis runs over, the one named last changes fastest.
Arguments:
- psi: float32 [16384, 640], P(('frag', 'grid')), parts along dimension 0
- order: int32 [10], P('frag'), parts along dimension 0, may hold values from 0 to 4, each once
Outputs:
- orthonormal: float32 [16384, 640], P(('frag', 'grid')), parts along dimension 0
There are 2 independent parts, one for each index of `frag`. A program takes and returns all parts, laid end to end along the dimension named above; each array names one. Nothing has to cross between parts.
All inputs are finite; a program needn't handle non-finite values.
Results may differ from a plain program's by a relative error of at most 0.00012.
Values sent between devices are 32-bit elements; how exact they have to be, the bound alone decides.
A program may use at most 64 MiB of HBM per device.

v0:
```python
import jax
import jax.numpy as jnp
from jax import lax
from jax.sharding import PartitionSpec as P

BLOCK = 128
NBLK = 5


def contract(left, right):
    return lax.dot_general(
        left,
        right,
        (((0,), (0,)), ((), ())),
        precision=lax.Precision.HIGHEST,
        preferred_element_type=jnp.float32,
    )


def matmul(left, right):
    return jnp.dot(left, right, precision=lax.Precision.HIGHEST, preferred_element_type=jnp.float32)


def factor_inverse(gram, width):
    lower = jnp.linalg.cholesky(gram)
    return lax.linalg.triangular_solve(
        lower, jnp.eye(width, dtype=gram.dtype), left_side=True, lower=True
    )


def local(psi, order):
    scale = jnp.float32(1.0 / (psi.shape[0] * lax.axis_size("grid")))
    rows = psi.shape[0]
    reordered = jnp.take(psi.reshape(rows, NBLK, BLOCK), order, axis=1).reshape(rows, NBLK * BLOCK)
    whole = lax.psum(contract(reordered, reordered) * scale, "grid")
    inverse = factor_inverse(whole, NBLK * BLOCK)
    basis = matmul(reordered, inverse.T).reshape(rows, NBLK, BLOCK)
    result = jnp.zeros((rows, NBLK, BLOCK), psi.dtype).at[:, order, :].set(basis)
    return result.reshape(rows, NBLK * BLOCK)


def solution(mesh):
    in_specs = (P(("frag", "grid"), None), P("frag"))
    out_specs = P(("frag", "grid"), None)
    return jax.shard_map(local, mesh=mesh, in_specs=in_specs, out_specs=out_specs, check_vma=False)
```

profile of v0, /device:TPU:0, one launch (start us, length us, event | category | flops | bytes accessed | tf_op | source)
XLA Modules:
  0.0 329.6 jit_solution(3840453212950638409)
XLA Ops:
  6.5 0.7 compare_select_fusion
  7.2 0.7 compare_and_fusion
  7.9 1.7 copy.5
  9.6 0.4 copy.6
  10.0 0.6 gather_fusion
  10.6 1.2 select_bitcast_fusion
  11.9 1.7 copy.7
  13.6 4.5 %convolution_multiply_fusion = f32[640,640]{0,1:T(8,128)} fusion(f32[512,640]{0,1:T(8,128)S(1)} %bitcast.79), kind=kOutput, calls=%fused_computation.9 | convolution fusion | flops 2516992000 | bytes 2949120 | tf_op jit(solution)/shard_map/dot_general | solution.py:11
  18.1 0.9 iota_compare_fusion
  19.0 1.3 fusion.20
  20.2 97.1 %all-reduce.3.cloned.1.call-done = f32[640,640]{0,1:T(8,128)} async-done(((f32[640,640]{0,1:T(8,128)}), f32[640,640]{0,1:T(8,128)}) %all-reduce.3.cloned.1.call-update) | async-done | bytes 1638416 | tf_op jit(solution)/shard_map/psum | solution.py:35
  117.3 3.0 copy.9
  120.3 1.6 fusion
  121.9 1.2 copy-done.1
  123.1 11.7 %cholesky.133 = f32[128,128]{1,0:T(8,128)S(1)} custom-call(f32[128,128]{1,0:T(8,128)S(1)} %cholesky.340), custom_call_target="Cholesky" | custom-call | tf_op jit(solution)/shard_map/jit(cholesky)/cholesky | solution.py:25
  134.9 9.8 %custom-call.38 = f32[1,128,128]{1,2,0:T(8,128)S(1)} custom-call(f32[1,128,128]{2,1,0:T(8,128)S(1)} %get-tuple-element.35), custom_call_target="InvertDiagBlocksLowerTriangular" | custom-call | tf_op jit(solution)/shard_map/jit(cholesky)/cholesky | solution.py:25
  144.7 0.1 cholesky.279
  144.8 1.3 constant_dynamic-update-slice_fusion.8
  146.1 1.3 convolution_subtract_fusion.3
  147.5 11.7 %cholesky.272 = f32[128,128]{1,0:T(8,128)S(1)} custom-call(f32[128,128]{1,0:T(8,128)S(1)} %cholesky.344), custom_call_target="Cholesky" | custom-call | tf_op jit(solution)/shard_map/jit(cholesky)/cholesky | solution.py:25
  159.2 10.0 %custom-call.39 = f32[1,128,128]{1,2,0:T(8,128)S(1)} custom-call(f32[1,128,128]{2,1,0:T(8,128)S(1)} %get-tuple-element.32), custom_call_target="InvertDiagBlocksLowerTriangular" | custom-call | tf_op jit(solution)/shard_map/jit(cholesky)/cholesky | solution.py:25
  169.2 0.3 convolution_dynamic-update-slice_fusion.1
  169.5 1.4 convolution_subtract_fusion.4
  171.0 11.7 %cholesky.293 = f32[128,128]{1,0:T(8,128)S(1)} custom-call(f32[128,128]{1,0:T(8,128)S(1)} %cholesky.349), custom_call_target="Cholesky" | custom-call | tf_op jit(solution)/shard_map/jit(cholesky)/cholesky | solution.py:25
  182.7 0.6 compare_reduce_fusion.2
  183.4 9.8 %custom-call.40 = f32[1,128,128]{1,2,0:T(8,128)S(1)} custom-call(f32[1,128,128]{2,1,0:T(8,128)S(1)} %get-tuple-element.29), custom_call_target="InvertDiagBlocksLowerTriangular" | custom-call | tf_op jit(solution)/shard_map/jit(cholesky)/cholesky | solution.py:25
  193.2 0.3 convolution_dynamic-update-slice_fusion.2
  193.4 1.4 convolution_subtract_fusion.5
  194.8 12.1 %cholesky.312 = f32[128,128]{1,0:T(8,128)S(1)} custom-call(f32[128,128]{1,0:T(8,128)S(1)} %cholesky.354), custom_call_target="Cholesky" | custom-call | tf_op jit(solution)/shard_map/jit(cholesky)/cholesky | solution.py:25
  207.0 0.7 compare_reduce_fusion.1
  207.6 9.8 %custom-call.41 = f32[1,128,128]{1,2,0:T(8,128)S(1)} custom-call(f32[1,128,128]{2,1,0:T(8,128)S(1)} %get-tuple-element.26), custom_call_target="InvertDiagBlocksLowerTriangular" | custom-call | tf_op jit(solution)/shard_map/jit(cholesky)/cholesky | solution.py:25
  217.5 0.2 convolution_dynamic-update-slice_fusion.3
  217.7 1.2 convolution_subtract_fusion.6
  218.9 11.7 %cholesky.329 = f32[128,128]{1,0:T(8,128)S(1)} custom-call(f32[128,128]{1,0:T(8,128)S(1)} %convolution_subtract_fusion.6), custom_call_target="Cholesky" | custom-call | tf_op jit(solution)/shard_map/jit(cholesky)/cholesky | solution.py:25
  230.6 0.7 compare_reduce_fusion
  231.3 0.7 compare_reduce_fusion.3
  235.1 1.3 select_select_fusion
  236.4 17.1 %while.1 = (s32[]{:T(128)}, f32[640,640]{1,0:T(8,128)}, s32[5,2]{0,1:T(2,128)S(1)}, f32[5,128,128]{2,1,0:T(8,128)}, s32[]{:T(128)}) while((s32[]{:T(128)}, f32[640,640]{1,0:T(8,128)}, s32[5,2]{0,1:T(2,128)S(1)}, f32[5,128,128]{2,1,0:T(8,128)}, s32[]{:T(128)}) %tuple.33), condition=%wide.while_cond, body=%wide.while_body.sunk | while | flops 2 | bytes 132705 | solution.py:26
  236.4 0.1 constant_dynamic-slice_fusion.2
  236.4 0.5 fusion.60
  237.0 2.8 bitcast_dynamic-update-slice_fusion.2
  239.9 0.5 fusion.60
  240.4 2.8 bitcast_dynamic-update-slice_fusion.2
  243.3 0.5 fusion.60
  243.8 2.8 bitcast_dynamic-update-slice_fusion.2
  246.7 0.5 fusion.60
  247.3 2.8 bitcast_dynamic-update-slice_fusion.2
  250.1 0.5 fusion.60
  250.7 2.7 bitcast_dynamic-update-slice_fusion.2
  253.4 50.2 %custom-call.42 = f32[5,128,128]{1,2,0:T(8,128)S(1)} custom-call(f32[5,128,128]{2,1,0:T(8,128)} %get-tuple-element.12), custom_call_target="InvertDiagBlocksLowerTriangular" | custom-call | tf_op jit(solution)/shard_map/triangular_solve | solution.py:26
  303.7 1.1 constant_dynamic-update-slice_fusion.3
  304.8 1.4 convolution_subtract_fusion.1
  306.3 0.5 constant_dynamic-update-slice_fusion.2
  306.7 1.4 convolution_subtract_fusion
  308.2 0.5 constant_dynamic-update-slice_fusion.1
  308.6 1.8 convolution_subtract_fusion.2
  310.5 0.5 constant_dynamic-update-slice_fusion
  310.9 1.9 fusion.9
  312.8 0.5 convolution_dynamic-update-slice_fusion
  313.3 6.4 %convolution_bitcast_fusion = f32[5,512,128]{2,1,0:T(8,128)S(1)} fusion(f32[512,640,1]{0,1,2:T(8,128)S(1)} %bitcast.80, f32[5,128,640]{2,1,0:T(8,128)S(1)} %bitcast.83), kind=kOutput, calls=%fused_computation.10 | convolution fusion | flops 2516582400 | bytes 4259840 | tf_op jit(solution)/shard_map/dot_general | solution.py:21
  319.7 0.1 broadcast_in_dim.18
  319.8 0.9 scatter_fusion
  320.7 0.4 copy.11
  321.1 1.5 copy.12
  (24 shorter events, 0.5 us)
Async XLA Ops:
  6.5 110.8 %all-reduce.3.cloned.1.call-start = ((), (), s32[]{:S(2)}) async-start(), calls=%async_computation | async-start | bytes 3276800 | tf_op jit(solution)/shard_map/psum | solution.py:35
  117.3 3.0 copy-start
  121.9 1.2 copy-start.1
  253.4 53.3 %copy-start.2 = (f32[640,640]{1,0:T(8,128)S(1)}, f32[640,640]{1,0:T(8,128)}, u32[]{:S(2)}) copy-start(f32[640,640]{1,0:T(8,128)} %fusion.20) | copy-start | bytes 4915204
Sparse Core Ops, SparseCore 0:
  18.2 99.0 all-reduce.2
where the time goes:
time: 334 us; the launch traced here: 330 us
  other arithmetic  159 us (48%)
  waiting for transfers between devices  97.1 us (29%)
  local copies, waits for them, and re-layouts  28.7 us (9%)
  matrix products  27.8 us (8%)
  between operations  16.9 us (5%)
    another operation x18, other arithmetic, factor_inverse(): lower = jnp.linalg.cholesky(gram)  101 us
    psum x1, waiting for transfers between devices, local(): whole = lax.psum(contract(reordered, reordered) * scale, 'grid')  97.1 us
    another operation x3, other arithmetic, factor_inverse(): lax.linalg.triangular_solve(lower, jnp.eye(width, dtype=gram.dtype), left...  51.5 us
    another operation x15, local copies, waits for them, and re-layouts  17.1 us
    another operation x9, matrix products, factor_inverse(): lax.linalg.triangular_solve(lower, jnp.eye(width, dtype=gram.dtype), left...  9.56 us
    another operation x8, matrix products, factor_inverse(): lower = jnp.linalg.cholesky(gram)  7.43 us
  transfers between devices with their start and end apart: 1, of which 1 were waited for; matrix products, arithmetic and copies ran while one was open for 1% of the time, Pallas kernels for 0%

commit v1 on v0

--- a/solution.py
+++ b/solution.py
@@ -32,7 +32,7 @@
     scale = jnp.float32(1.0 / (psi.shape[0] * lax.axis_size("grid")))
     rows = psi.shape[0]
     reordered = jnp.take(psi.reshape(rows, NBLK, BLOCK), order, axis=1).reshape(rows, NBLK * BLOCK)
-    whole = lax.psum(contract(reordered, reordered) * scale, "grid")
+    whole = jnp.sum(lax.all_gather(contract(reordered, reordered) * scale, "grid"), axis=0)
     inverse = factor_inverse(whole, NBLK * BLOCK)
     basis = matmul(reordered, inverse.T).reshape(rows, NBLK, BLOCK)
     result = jnp.zeros((rows, NBLK, BLOCK), psi.dtype).at[:, order, :].set(basis)

time: 334 us -> 382 us (1.14)
  waiting for transfers between devices: 97.1 us -> 134 us
  other arithmetic: 159 us -> 170 us
    all_gather x0 -> x1, waiting for transfers between devices: none -> 134 us  [local(): lax.all_gather(contract(reordered, reordered) * scale, 'grid')]
    psum x1 -> x0, waiting for transfers between devices: 97.1 us -> none  [local(): whole = lax.psum(contract(reordered, reordered) * scale, 'grid')]
    reduce_sum x0 -> x1, other arithmetic: none -> 10.5 us  [local(): jnp.sum(lax.all_gather(contract(reordered, reordered) * scale, 'grid'), a...]
where the time goes in v1:
time: 382 us; the launch traced here: 377 us
  other arithmetic  170 us (45%)
  waiting for transfers between devices  134 us (35%)
  local copies, waits for them, and re-layouts  27.9 us (7%)
  matrix products  27.8 us (7%)
  between operations  17.1 us (4%)
    all_gather x1, waiting for transfers between devices, local(): lax.all_gather(contract(reordered, reordered) * scale, 'grid')  134 us
    another operation x18, other arithmetic, factor_inverse(): lower = jnp.linalg.cholesky(gram)  101 us
    another operation x3, other arithmetic, factor_inverse(): lax.linalg.triangular_solve(lower, jnp.eye(width, dtype=gram.dtype), left...  51.6 us
    another operation x15, local copies, waits for them, and re-layouts  17.5 us
    reduce_sum x1, other arithmetic, local(): jnp.sum(lax.all_gather(contract(reordered, reordered) * scale, 'grid'), a...  10.5 us
    another operation x9, matrix products, factor_inverse(): lax.linalg.triangular_solve(lower, jnp.eye(width, dtype=gram.dtype), left...  9.56 us
  transfers between devices with their start and end apart: 1, of which 1 were waited for; matrix products, arithmetic and copies ran while one was open for 1% of the time, Pallas kernels for 0%

profile of v1, /device:TPU:0, one launch (start us, length us, event | category | flops | bytes accessed | tf_op | source)
XLA Modules:
  0.0 376.6 jit_solution(6757151556197636187)
XLA Ops:
  6.5 0.7 compare_select_fusion
  7.2 0.7 compare_and_fusion
  7.9 1.7 copy.11
  9.6 0.4 copy.12
  10.0 0.6 gather_fusion
  10.6 1.2 select_bitcast_fusion
  11.9 1.7 copy.13
  13.6 4.5 %convolution_multiply_fusion = f32[640,640]{1,0:T(8,128)} fusion(f32[512,640]{0,1:T(8,128)S(1)} %bitcast.81), kind=kOutput, calls=%fused_computation.9 | convolution fusion | flops 2516992000 | bytes 2949120 | tf_op jit(solution)/shard_map/dot_general | solution.py:11
  18.1 0.9 iota_compare_fusion
  19.0 1.3 fusion.20
  20.3 134.2 %all-gather.3.cloned.1.call-done = f32[10240,640]{1,0:T(8,128)} async-done(((f32[640,640]{1,0:T(8,128)}), f32[10240,640]{1,0:T(8,128)}) %all-gather.3.cloned.1.call-update) | async-done | bytes 26214416 | tf_op jit(solution)/shard_map/all_gather | solution.py:35
  154.4 10.5 %reduce_sum.9 = f32[640,640]{1,0:T(8,128)S(1)} reduce(f32[16,640,640]{2,1,0:T(8,128)} %bitcast.80, f32[]{:T(128)} %constant.184.clone.1), dimensions={0}, to_apply=%region_0.1 | reduce | flops 6144000 | bytes 27852804 | tf_op jit(solution)/shard_map/reduce_sum | solution.py:35
  164.9 1.9 copy.14
  166.8 1.6 fusion
  168.4 1.2 copy-done
  169.6 11.7 %cholesky.133 = f32[128,128]{1,0:T(8,128)S(1)} custom-call(f32[128,128]{1,0:T(8,128)S(1)} %cholesky.340), custom_call_target="Cholesky" | custom-call | tf_op jit(solution)/shard_map/jit(cholesky)/cholesky | solution.py:25
  181.3 0.1 cholesky.279
  181.4 9.8 %custom-call.38 = f32[1,128,128]{1,2,0:T(8,128)S(1)} custom-call(f32[1,128,128]{2,1,0:T(8,128)S(1)} %get-tuple-element.35), custom_call_target="InvertDiagBlocksLowerTriangular" | custom-call | tf_op jit(solution)/shard_map/jit(cholesky)/cholesky | solution.py:25
  191.2 1.3 constant_dynamic-update-slice_fusion.8
  192.6 1.3 convolution_subtract_fusion.3
  193.9 11.7 %cholesky.272 = f32[128,128]{1,0:T(8,128)S(1)} custom-call(f32[128,128]{1,0:T(8,128)S(1)} %cholesky.344), custom_call_target="Cholesky" | custom-call | tf_op jit(solution)/shard_map/jit(cholesky)/cholesky | solution.py:25
  205.7 10.0 %custom-call.39 = f32[1,128,128]{1,2,0:T(8,128)S(1)} custom-call(f32[1,128,128]{2,1,0:T(8,128)S(1)} %get-tuple-element.32), custom_call_target="InvertDiagBlocksLowerTriangular" | custom-call | tf_op jit(solution)/shard_map/jit(cholesky)/cholesky | solution.py:25
  215.7 0.3 convolution_dynamic-update-slice_fusion.1
  216.0 1.4 convolution_subtract_fusion.4
  217.4 11.7 %cholesky.293 = f32[128,128]{1,0:T(8,128)S(1)} custom-call(f32[128,128]{1,0:T(8,128)S(1)} %cholesky.349), custom_call_target="Cholesky" | custom-call | tf_op jit(solution)/shard_map/jit(cholesky)/cholesky | solution.py:25
  229.1 0.7 compare_reduce_fusion.2
  229.8 9.8 %custom-call.40 = f32[1,128,128]{1,2,0:T(8,128)S(1)} custom-call(f32[1,128,128]{2,1,0:T(8,128)S(1)} %get-tuple-element.29), custom_call_target="InvertDiagBlocksLowerTriangular" | custom-call | tf_op jit(solution)/shard_map/jit(cholesky)/cholesky | solution.py:25
  239.6 0.3 convolution_dynamic-update-slice_fusion.2
  239.9 1.4 convolution_subtract_fusion.5
  241.3 12.1 %cholesky.312 = f32[128,128]{1,0:T(8,128)S(1)} custom-call(f32[128,128]{1,0:T(8,128)S(1)} %cholesky.354), custom_call_target="Cholesky" | custom-call | tf_op jit(solution)/shard_map/jit(cholesky)/cholesky | solution.py:25
  253.4 0.7 compare_reduce_fusion.1
  254.1 9.8 %custom-call.41 = f32[1,128,128]{1,2,0:T(8,128)S(1)} custom-call(f32[1,128,128]{2,1,0:T(8,128)S(1)} %get-tuple-element.26), custom_call_target="InvertDiagBlocksLowerTriangular" | custom-call | tf_op jit(solution)/shard_map/jit(cholesky)/cholesky | solution.py:25
  263.9 0.2 convolution_dynamic-update-slice_fusion.3
  264.1 1.2 convolution_subtract_fusion.6
  265.4 11.7 %cholesky.329 = f32[128,128]{1,0:T(8,128)S(1)} custom-call(f32[128,128]{1,0:T(8,128)S(1)} %convolution_subtract_fusion.6), custom_call_target="Cholesky" | custom-call | tf_op jit(solution)/shard_map/jit(cholesky)/cholesky | solution.py:25
  277.1 0.7 compare_reduce_fusion
  277.8 0.7 compare_reduce_fusion.3
  281.7 1.3 select_select_fusion
  283.0 17.5 %while.1 = (s32[]{:T(128)}, f32[640,640]{1,0:T(8,128)}, s32[5,2]{0,1:T(2,128)S(1)}, f32[5,128,128]{2,1,0:T(8,128)}, s32[]{:T(128)}) while((s32[]{:T(128)}, f32[640,640]{1,0:T(8,128)}, s32[5,2]{0,1:T(2,128)S(1)}, f32[5,128,128]{2,1,0:T(8,128)}, s32[]{:T(128)}) %tuple.33), condition=%wide.while_cond, body=%wide.while_body.sunk | while | flops 2 | bytes 132705 | solution.py:26
  283.0 0.5 fusion.60
  283.6 2.9 bitcast_dynamic-update-slice_fusion.2
  286.6 0.5 fusion.60
  287.1 2.9 bitcast_dynamic-update-slice_fusion.2
  290.1 0.5 fusion.60
  290.6 2.9 bitcast_dynamic-update-slice_fusion.2
  293.6 0.5 fusion.60
  294.1 2.9 bitcast_dynamic-update-slice_fusion.2
  297.1 0.5 fusion.60
  297.6 2.8 bitcast_dynamic-update-slice_fusion.2
  300.5 50.2 %custom-call.42 = f32[5,128,128]{1,2,0:T(8,128)S(1)} custom-call(f32[5,128,128]{2,1,0:T(8,128)} %get-tuple-element.12), custom_call_target="InvertDiagBlocksLowerTriangular" | custom-call | tf_op jit(solution)/shard_map/triangular_solve | solution.py:26
  350.7 1.1 constant_dynamic-update-slice_fusion.3
  351.8 1.4 convolution_subtract_fusion.1
  353.3 0.5 constant_dynamic-update-slice_fusion.2
  353.8 1.4 convolution_subtract_fusion
  355.2 0.5 constant_dynamic-update-slice_fusion.1
  355.7 1.8 convolution_subtract_fusion.2
  357.5 0.5 constant_dynamic-update-slice_fusion
  357.9 1.9 fusion.9
  359.9 0.5 convolution_dynamic-update-slice_fusion
  360.3 6.4 %convolution_bitcast_fusion = f32[5,512,128]{2,1,0:T(8,128)S(1)} fusion(f32[512,640,1]{0,1,2:T(8,128)S(1)} %bitcast.82, f32[5,128,640]{2,1,0:T(8,128)S(1)} %bitcast.85), kind=kOutput, calls=%fused_computation.10 | convolution fusion | flops 2516582400 | bytes 4259840 | tf_op jit(solution)/shard_map/dot_general | solution.py:21
  366.7 0.1 broadcast_in_dim.18
  366.8 0.9 scatter_fusion
  367.7 0.4 copy.16
  368.1 1.5 copy.17
  (23 shorter events, 0.6 us)
Async XLA Ops:
  6.5 147.9 %all-gather.3.cloned.1.call-start = ((), (), s32[]{:S(2)}) async-start(), calls=%async_computation | async-start | bytes 27852800 | tf_op jit(solution)/shard_map/all_gather | solution.py:35
  168.4 1.2 copy-start
  300.5 53.3 %copy-start.1 = (f32[640,640]{1,0:T(8,128)S(1)}, f32[640,640]{1,0:T(8,128)}, u32[]{:S(2)}) copy-start(f32[640,640]{1,0:T(8,128)} %fusion.20) | copy-start | bytes 4915204
Sparse Core Ops, SparseCore 0:
  18.2 136.1 all-gather.2
